TPU v7x, 256 devices: a 4x2x16 block of a 4x16x16 slice. The times are simulated.
256 devices in a mesh: groups: 2 (over y), ctx: 128 (over x, z, core).
Axes of the slice: x: 4, y: 2, z: 16, core: 2. Of those that a mesh axis runs over, the one named last changes fastest.
The devices are a block of a 4x16x16 slice.
Arguments:
- prompt_query: bfloat16 [16384, 4096], P(('groups', 'ctx')), parts along dimension 0, may hold values from -6 to 6
- prompt_key: bfloat16 [16384, 512], P(('groups', 'ctx')), parts along dimension 0, may hold values from -6 to 6
- prompt_value: bfloat16 [16384, 512], P(('groups', 'ctx')), parts along dimension 0, may hold values from -6 to 6
- prefix_key_cache: bfloat16 [2048, 512], P(('groups', 'ctx')), parts along dimension 0, may hold values from -6 to 6
- prefix_value_cache: bfloat16 [2048, 512], P(('groups', 'ctx')), parts along dimension 0, may hold values from -6 to 6
- decoded_query: bfloat16 [8192], P('groups'), parts along dimension 0, may hold values from -6 to 6
- decoded_key: bfloat16 [1024], P('groups'), parts along dimension 0, may hold values from -6 to 6
- decoded_value: bfloat16 [1024], P('groups'), parts along dimension 0, may hold values from -6 to 6
- shard_counts: int32 [256, 2], P('groups'), parts along dimension 0, may hold values from 0 to 32, as said below
- block_offsets: int32 [256, 2], P('groups'), parts along dimension 0, may hold values from 0 to 8160, as said below
Outputs:
- span_out: bfloat16 [16384, 4096], P(('groups', 'ctx')), parts along dimension 0
- next_out: bfloat16 [8192], P('groups'), parts along dimension 0
There are 2 independent parts, one for each index of `groups`. A program takes and returns all parts, laid end to end along the dimension named above; each array names one. Nothing has to cross between parts.
Inputs may be any that keep to these rules, and one draw needn't show every extreme that they name: block_offsets[i, 0] = 32 * p_i and block_offsets[i, 1] = 32 * (255 - p_i) for a permutation p of 0 to 127. shard_counts[i, h] = min(32, max(0, L - block_offsets[i, h])) for one prompt length L with 4096 < L <= 8128.
All inputs are finite; a program needn't handle non-finite values.
Results may differ from a plain program's by a relative error of at most 0.0055.
Values may be sent and summed in bfloat16 or wider, within the bound.
No kernel may reach another device: no remote copies, remote signals or barrier semaphores. Data moves between devices by JAX's collectives and lax.ppermute only.
A program may use at most 128 MiB of HBM per device.

v0:
```python
import functools

import jax
import jax.numpy as jnp
from jax import lax
from jax.experimental import pallas as pl
from jax.experimental.pallas import tpu as pltpu
from jax.sharding import Mesh
from jax.sharding import PartitionSpec as P

KEY_VALUE_HEADS = 4
HEAD_WIDTH = 128
HEADS_PER_GROUP = 8
GROUP_WIDTH = HEADS_PER_GROUP * HEAD_WIDTH
CTX = ("ctx_0", "ctx_1", "ctx_2")
GROUPS_CTX = ("groups", "ctx_0", "ctx_1", "ctx_2")
RING = ("ctx_1", "ctx_2")
COLUMNS = KEY_VALUE_HEADS
CORES = 2
HALF = 32
PREFIX = 8
LOW = COLUMNS * HALF
NEAR = LOW + COLUMNS * PREFIX
BLOCK = NEAR + LOW
TILES = 2 * COLUMNS
TILE = HALF * HEADS_PER_GROUP
NEGATIVE_FILL = -1e30
EXP2_SCALE = HEAD_WIDTH**-0.5 * 1.4426950408889634
NT = (((1,), (1,)), ((), ()))


def source_index(where_ref, column, ring_step, flip, depth):
    x, z, core = where_ref[0], where_ref[1], where_ref[2]
    way = jnp.where(core == 0, -ring_step, ring_step)
    if flip[0]:
        way = -way
    z_from = lax.rem(z + way + depth, depth)
    core_from = 1 - core if flip[1] else core
    x_from = lax.rem(x - column + COLUMNS, COLUMNS)
    return (x_from * depth + z_from) * CORES + core_from


def attention_step(
    where_ref, offset_ref, count_ref, *refs, flips, depth, first, last
):
    if len(flips) == 4:
        near_first, near_second, far = refs[:3]
        blocks = (near_first, near_second, far.at[:BLOCK], far.at[BLOCK:])
        refs = refs[3:]
    else:
        blocks, refs = refs[: len(flips)], refs[len(flips) :]
    query_ref, decode_query_ref = refs[:2]
    refs = refs[2:]
    if last:
        decode_key_ref, decode_value_ref = refs[:2]
        refs = refs[2:]
    if not first:
        acc_in, stats_in, decode_in = refs[:3]
        refs = refs[3:]
    if last:
        out_ref = refs[0]
        refs = refs[1:]
    else:
        acc_out, stats_out, decode_out = refs[:3]
        refs = refs[3:]
    keys, values_t, *tiles, pending = refs
    score_refs, weight_refs, peak_refs = tiles[:2], tiles[2:4], tiles[4:]

    count = len(flips)
    near, total = count * NEAR, count * BLOCK
    for b, block in enumerate(blocks):
        keys[b * NEAR : (b + 1) * NEAR, :] = block[:NEAR, :HEAD_WIDTH]
        keys[near + b * LOW : near + (b + 1) * LOW, :] = block[NEAR:, :HEAD_WIDTH]
    values = jnp.concatenate(
        [block[:NEAR, HEAD_WIDTH:] for block in blocks]
        + [block[NEAR:, HEAD_WIDTH:] for block in blocks],
        0,
    )
    values_t[...] = values.T

    ring_step = where_ref[3]
    sources = [
        [source_index(where_ref, j, ring_step, flip, depth) for j in range(COLUMNS)]
        for flip in flips
    ]
    bounds = (near, total)
    if first:
        spread = lax.broadcasted_iota(jnp.int32, (HALF, TILE), 0) - lax.rem(
            lax.broadcasted_iota(jnp.int32, (HALF, TILE), 1), HALF
        )

    def pieces(column, half):
        own = source_index(where_ref, column, 0, (False, False), depth)
        base = offset_ref[own * 2 + half]
        found = []
        for b in range(count):
            at = b * NEAR
            for j in range(COLUMNS):
                gap = None if half else base - offset_ref[sources[b][j] * 2]
                found.append((at + j * HALF, HALF, gap))
            found.append((at + LOW, NEAR - LOW, None))
        if half:
            for b in range(count):
                for j in range(COLUMNS):
                    gap = base - offset_ref[sources[b][j] * 2 + 1]
                    found.append((near + b * LOW + j * HALF, HALF, gap))
        return found

    def score(column, half):
        rows = bounds[half]
        query = jnp.concatenate(
            [
                query_ref[column, half * HALF : (half + 1) * HALF, h * HEAD_WIDTH : (h + 1) * HEAD_WIDTH]
                for h in range(HEADS_PER_GROUP)
            ],
            0,
        )
        scores = lax.dot_general(keys[:rows, :], query, NT, preferred_element_type=jnp.float32)
        peak = jnp.full((8, TILE), NEGATIVE_FILL, jnp.float32)
        for at, size, gap in pieces(column, half):
            part = scores[at : at + size, :]
            if first and gap is not None:
                part = jnp.where(spread <= gap, part, NEGATIVE_FILL)
            score_refs[half][at : at + size, :] = part
            top = jnp.max(part.reshape(size // 8, 8, TILE), axis=0)
            if gap is not None and not first:
                top = jnp.where(gap > 0, top, NEGATIVE_FILL)
            peak = jnp.maximum(peak, top)
        peak_refs[half][...] = peak

    def weigh(column, half):
        tile = column * 2 + half
        peak = jnp.max(peak_refs[half][...], axis=0, keepdims=True)
        if not first:
            old_peak = stats_in[tile, 0:1, :]
            peak = jnp.maximum(peak, old_peak)
        peak8 = jnp.broadcast_to(peak, (8, TILE))
        totals = jnp.zeros((8, TILE), jnp.float32)
        for at, size, gap in pieces(column, half):
            level = peak8
            if gap is not None and not first:
                level = jnp.where(gap > 0, peak8, -NEGATIVE_FILL)
            part = score_refs[half][at : at + size, :].reshape(size // 8, 8, TILE)
            weights = jnp.exp2((part - level[None]) * EXP2_SCALE)
            totals = totals + jnp.sum(weights, axis=0)
            weight_refs[half][at : at + size, :] = weights.reshape(size, TILE).astype(jnp.bfloat16)
        totals = jnp.sum(totals, axis=0, keepdims=True)
        if not first:
            rescale = jnp.exp2((old_peak - peak) * EXP2_SCALE)
            totals = totals + rescale * stats_in[tile, 1:2, :]
            pending[half, 0:1, :] = rescale
        if last:
            pending[half, 1:2, :] = totals
        else:
            stats_out[tile, 0:1, :] = peak
            stats_out[tile, 1:2, :] = totals

    def mix(column, half, tile):
        rows = bounds[half]
        mixture = jnp.dot(
            values_t[:, :rows], weight_refs[half][...], preferred_element_type=jnp.float32
        )
        if not first:
            mixture = mixture + pending[half, 0:1, :] * acc_in[tile]
        if last:
            own = source_index(where_ref, column, 0, (False, False), depth)
            live = count_ref[own * 2 + half]
            slot = lax.rem(lax.broadcasted_iota(jnp.int32, (1, TILE), 1), HALF)
            factor = jnp.where(slot < live, 1.0 / pending[half, 1:2, :], 0.0)
            result = (mixture * factor).T.astype(jnp.bfloat16)
            for h in range(HEADS_PER_GROUP):
                out_ref[column, half * HALF : (half + 1) * HALF, h * HEAD_WIDTH : (h + 1) * HEAD_WIDTH] = (
                    result[h * HALF : (h + 1) * HALF, :]
                )
        else:
            acc_out[tile] = mixture

    score(0, 0)

    def column_step(column, carry):
        before = jnp.maximum(column - 1, 0)
        mix(before, 1, jnp.where(column == 0, TILES, before * 2 + 1))
        score(column, 1)
        weigh(column, 0)
        mix(column, 0, column * 2)
        score(jnp.minimum(column + 1, COLUMNS - 1), 0)
        weigh(column, 1)
        return carry

    lax.fori_loop(0, COLUMNS, column_step, 0)
    mix(COLUMNS - 1, 1, TILES - 1)

    scores = lax.dot_general(
        decode_query_ref[...], keys[...], NT, preferred_element_type=jnp.float32
    )
    lane = lax.broadcasted_iota(jnp.int32, (1, total), 1)
    live = jnp.full((1, total), HALF, jnp.int32)
    for b in range(count):
        for j in range(COLUMNS):
            at = near + b * LOW + j * HALF
            live = jnp.where(
                (lane >= at) & (lane < at + HALF), count_ref[sources[b][j] * 2 + 1], live
            )
    scores = jnp.where(lax.rem(lane, HALF) < live, scores, NEGATIVE_FILL)
    peak = jnp.max(scores, axis=1, keepdims=True)
    if not first:
        old_peak = decode_in[:, HEAD_WIDTH : HEAD_WIDTH + 1]
        peak = jnp.maximum(peak, old_peak)
    weights = jnp.exp2((scores - peak) * EXP2_SCALE)
    totals = jnp.sum(weights, axis=1, keepdims=True)
    mixture = lax.dot_general(
        weights.astype(jnp.bfloat16), values_t[...], NT, preferred_element_type=jnp.float32
    )
    if not first:
        rescale = jnp.exp2((old_peak - peak) * EXP2_SCALE)
        totals = totals + rescale * decode_in[:, 2 * HEAD_WIDTH : 2 * HEAD_WIDTH + 1]
        mixture = mixture + rescale * decode_in[:, :HEAD_WIDTH]
    if last:
        query = decode_query_ref[...].astype(jnp.float32)
        own_score = jnp.sum(
            query * decode_key_ref[...].astype(jnp.float32), axis=1, keepdims=True
        )
        top = jnp.maximum(peak, own_score)
        keep = jnp.exp2((peak - top) * EXP2_SCALE)
        own_weight = jnp.exp2((own_score - top) * EXP2_SCALE)
        numerator = keep * mixture + own_weight * decode_value_ref[...].astype(jnp.float32)
        result = numerator / (keep * totals + own_weight)
        for column in range(COLUMNS):
            for h in range(HEADS_PER_GROUP):
                out_ref[column, 2 * HALF : 2 * HALF + 8, h * HEAD_WIDTH : (h + 1) * HEAD_WIDTH] = (
                    jnp.broadcast_to(result[h : h + 1, :], (8, HEAD_WIDTH)).astype(jnp.bfloat16)
                )
    else:
        decode_out[:, :HEAD_WIDTH] = mixture
        decode_out[:, HEAD_WIDTH : 2 * HEAD_WIDTH] = jnp.broadcast_to(peak, mixture.shape)
        decode_out[:, 2 * HEAD_WIDTH :] = jnp.broadcast_to(totals, mixture.shape)


STATE = (
    jax.ShapeDtypeStruct((TILES + 1, HEAD_WIDTH, TILE), jnp.float32),
    jax.ShapeDtypeStruct((TILES, 8, TILE), jnp.float32),
    jax.ShapeDtypeStruct((16, 3 * HEAD_WIDTH), jnp.float32),
)


def run_step(offsets, counts, where, blocks, flips, depth, query, decode, state, last):
    first = state is None
    smem = pl.BlockSpec(memory_space=pltpu.SMEM)
    vmem = pl.BlockSpec(memory_space=pltpu.VMEM)
    operands = [where, offsets, counts, *blocks, query, decode[0]]
    if last:
        operands += decode[1:]
    aliases = {}
    if not first:
        if not last:
            aliases = {len(operands) + i: i for i in range(3)}
        operands += state
    near, total = len(flips) * NEAR, len(flips) * BLOCK
    if last:
        out_shape = jax.ShapeDtypeStruct((COLUMNS, 2 * HALF + 8, GROUP_WIDTH), jnp.bfloat16)
        out_specs = vmem
    else:
        out_shape, out_specs = STATE, (vmem,) * 3
    kernel = functools.partial(
        attention_step, flips=flips, depth=depth, first=first, last=last
    )
    return pl.pallas_call(
        kernel,
        out_shape=out_shape,
        in_specs=[smem] * 3 + [vmem] * (len(operands) - 3),
        out_specs=out_specs,
        scratch_shapes=[
            pltpu.VMEM((total, HEAD_WIDTH), jnp.bfloat16),
            pltpu.VMEM((HEAD_WIDTH, total), jnp.bfloat16),
            pltpu.VMEM((near, TILE), jnp.float32),
            pltpu.VMEM((total, TILE), jnp.float32),
            pltpu.VMEM((near, TILE), jnp.bfloat16),
            pltpu.VMEM((total, TILE), jnp.bfloat16),
            pltpu.VMEM((8, TILE), jnp.float32),
            pltpu.VMEM((8, TILE), jnp.float32),
            pltpu.VMEM((2, 8, TILE), jnp.float32),
        ],
        input_output_aliases=aliases,
        compiler_params=pltpu.CompilerParams(vmem_limit_bytes=12 << 20),
        cost_estimate=pl.CostEstimate(
            flops=total * TILES * TILE * HEAD_WIDTH * 4,
            bytes_accessed=4 << 20,
            transcendentals=total * TILES * TILE,
        ),
        name="attention_first" if first else "attention_last" if last else "attention",
    )(*operands)


def rotation(size, by):
    return [(i, (i + by) % size) for i in range(size)]


def body(
    prompt_query,
    prompt_key,
    prompt_value,
    prefix_key_cache,
    prefix_value_cache,
    decoded_query,
    decoded_key,
    decoded_value,
    shard_counts,
    block_offsets,
):
    depth = lax.axis_size("ctx_1")
    x, z, core = (lax.axis_index(a) for a in CTX)
    where = jnp.stack([x, z, core, jnp.zeros_like(x)]).astype(jnp.int32)
    offsets = block_offsets.reshape(-1)
    counts = shard_counts.reshape(-1)

    def key_value_of(head):
        keys = jnp.concatenate([prompt_key, prefix_key_cache], 0)
        values = jnp.concatenate([prompt_value, prefix_value_cache], 0)
        at = head * HEAD_WIDTH
        return jnp.concatenate(
            [
                lax.dynamic_slice_in_dim(keys, at, HEAD_WIDTH, 1),
                lax.dynamic_slice_in_dim(values, at, HEAD_WIDTH, 1),
            ],
            1,
        )

    def heads_at(by):
        return lax.rem(x + by, COLUMNS)

    parts = [key_value_of(x)]
    for by in range(1, COLUMNS):
        parts.append(lax.ppermute(key_value_of(heads_at(by)), "ctx_0", rotation(COLUMNS, by)))

    def query_of(head):
        return lax.dynamic_slice_in_dim(prompt_query, head * GROUP_WIDTH, GROUP_WIDTH, 1)

    queries = [query_of(x)]
    for by in range(1, COLUMNS):
        mine = query_of(heads_at(by))
        queries.append(lax.ppermute(mine, "ctx_0", rotation(COLUMNS, by)))

    own = jnp.concatenate(
        [p[:HALF] for p in parts] + [p[2 * HALF :] for p in parts] + [p[HALF : 2 * HALF] for p in parts],
        0,
    )
    query = jnp.stack(queries)

    def to_rows(vector, rows):
        part = lax.dynamic_slice_in_dim(vector.reshape(COLUMNS, -1), x, 1, 0)
        part = part.reshape(-1, HEAD_WIDTH)
        return jnp.concatenate([part, jnp.zeros((rows - part.shape[0], HEAD_WIDTH), part.dtype)], 0)

    decode_query = to_rows(decoded_query, 16)
    decode_key = lax.dynamic_slice_in_dim(decoded_key.reshape(COLUMNS, HEAD_WIDTH), x, 1, 0)
    decode_value = lax.dynamic_slice_in_dim(decoded_value.reshape(COLUMNS, HEAD_WIDTH), x, 1, 0)
    decode = [decode_query, decode_key, decode_value]

    ring = []
    for i in range(depth):
        ring.append((i * CORES, ((i + 1) % depth) * CORES))
        ring.append((i * CORES + 1, ((i - 1) % depth) * CORES + 1))

    def pass_on(block):
        return lax.ppermute(block, RING, ring)

    def swap(block):
        return lax.ppermute(block, "ctx_2", rotation(CORES, 1))

    step = functools.partial(run_step, offsets, counts, depth=depth, query=query, decode=decode)
    near_flips = ((False, False), (False, True))
    far_flips = ((True, True), (True, False))
    first, second = own, swap(own)
    state = None
    for s in range(depth // 2):
        blocks = [first, second]
        if s:
            blocks.append(swap(jnp.concatenate([first, second], 0)))
        state = step(
            where=where,
            blocks=blocks,
            flips=near_flips + far_flips if s else near_flips,
            state=state,
            last=False,
        )
        first = pass_on(first)
        if s + 1 < depth // 2:
            second = pass_on(second)
        where = lax.optimization_barrier(where + jnp.array([0, 0, 0, 1], jnp.int32))
    out = step(
        where=where,
        blocks=[first, swap(first)],
        flips=((False, False), (True, True)),
        state=state,
        last=True,
    )

    back = [out[0]]
    for by in range(1, COLUMNS):
        back.append(lax.ppermute(out[by], "ctx_0", rotation(COLUMNS, -by)))
    joined = jnp.concatenate(back + back[:-1], 1)
    joined = lax.dynamic_slice_in_dim(
        joined, lax.rem(COLUMNS - x, COLUMNS) * GROUP_WIDTH, COLUMNS * GROUP_WIDTH, 1
    )
    return joined[: 2 * HALF], joined[2 * HALF]


def solution(mesh):
    groups = mesh.shape["groups"]
    split = Mesh(
        mesh.devices.reshape(groups, COLUMNS, -1, CORES), ("groups", *CTX)
    )

    return jax.shard_map(
        body,
        mesh=split,
        in_specs=(
            P(GROUPS_CTX, None),
            P(GROUPS_CTX, None),
            P(GROUPS_CTX, None),
            P(GROUPS_CTX, None),
            P(GROUPS_CTX, None),
            P("groups"),
            P("groups"),
            P("groups"),
            P("groups", None),
            P("groups", None),
        ),
        out_specs=(P(GROUPS_CTX, None), P("groups")),
        check_vma=False,
    )
```

profile of v0, /device:TPU:33, one launch (start us, length us, event | category | flops | bytes accessed | tf_op | source)
XLA Modules:
  0.0 124.7 jit_solution(17145108394801741982)
XLA Ops:
  3.9 3.8 %collective-permute-start.2 = (bf16[72,256]{1,0:T(8,128)(2,1)S(1)}, bf16[72,256]{1,0:T(8,128)(2,1)S(1)}, u32[]{:S(2)}, u32[]{:S(2)}) collective-permute-start(bf16[72,256]{1,0:T(8,128)(2,1)S(1)} %pad_maximum_fusion.10), channel_id=1, source_target_pairs={{0,96},{32,0},{64,32},{96,64},{1,97},{33,1},{65,33},{97,65},{2,98}... | collective-permute-start | bytes 110600 | tf_op jit(solution)/shard_map/ppermute | solution.py:333
  8.7 3.7 %collective-permute-done = bf16[72,256]{1,0:T(8,128)(2,1)S(1)} collective-permute-done((bf16[72,256]{1,0:T(8,128)(2,1)S(1)}, bf16[72,256]{1,0:T(8,128)(2,1)S(1)}, u32[]{:S(2)}, u32[]{:S(2)}) %collective-permute-start) | collective-permute-done | bytes 36896 | tf_op jit(solution)/shard_map/ppermute | solution.py:333
  12.6 18.8 %collective-permute-start.15 = (bf16[288,256]{1,0:T(8,128)(2,1)S(1)}, bf16[288,256]{1,0:T(8,128)(2,1)S(1)}, u32[]{:S(2)}, u32[]{:S(2)}) collective-permute-start(bf16[288,256]{1,0:T(8,128)(2,1)S(1)} %constant_dynamic-update-slice_fusion.4.refs_0_), channel_id=1, source_target_pairs={{0,1},{1,0},{2,3},{3,2},{4,5},{5,4},{6,7},{7,6},{8,9},{9,8},{10,11... | collective-permute-start | bytes 442376 | tf_op jit(solution)/shard_map/ppermute | solution.py:368
  32.0 2.4 %collective-permute-start.13 = (bf16[64,1024]{1,0:T(8,128)(2,1)S(1)}, bf16[64,1024]{1,0:T(8,128)(2,1)S(1)}, u32[]{:S(2)}, u32[]{:S(2)}) collective-permute-start(bf16[64,1024]{1,0:T(8,128)(2,1)S(1)} %get-tuple-element.58), channel_id=1, source_target_pairs={{0,64},{32,96},{64,0},{96,32},{1,65},{33,97},{65,1},{97,33},{2,66}... | collective-permute-start | bytes 393224 | tf_op jit(solution)/shard_map/ppermute | solution.py:341
  34.6 5.8 %collective-permute-start.3 = (bf16[288,256]{1,0:T(8,128)(2,1)S(1)}, bf16[288,256]{1,0:T(8,128)(2,1)S(1)}, u32[]{:S(2)}, u32[]{:S(2)}) collective-permute-start(bf16[288,256]{1,0:T(8,128)(2,1)S(1)} %constant_dynamic-update-slice_fusion.4.refs_0_), channel_id=1, source_target_pairs={{0,2},{1,31},{2,4},{3,1},{4,6},{5,3},{6,8},{7,5},{8,10},{9,7},{10,... | collective-permute-start | bytes 442376 | tf_op jit(solution)/shard_map/ppermute | solution.py:365
  40.5 2.0 %collective-permute-done.3.refs_0_ = bf16[288,256]{1,0:T(8,128)(2,1)S(1)} collective-permute-done((bf16[288,256]{1,0:T(8,128)(2,1)S(1)}, bf16[288,256]{1,0:T(8,128)(2,1)S(1)}, u32[]{:S(2)}, u32[]{:S(2)}) %collective-permute-start.3) | collective-permute-done | bytes 147488 | tf_op jit(solution)/shard_map/ppermute | solution.py:365
  42.5 3.4 %collective-permute-start.4 = (bf16[288,256]{1,0:T(8,128)(2,1)S(1)}, bf16[288,256]{1,0:T(8,128)(2,1)S(1)}, u32[]{:S(2)}, u32[]{:S(2)}) collective-permute-start(bf16[288,256]{1,0:T(8,128)(2,1)S(1)} %collective-permute-done.3.refs_0_), channel_id=1, source_target_pairs={{0,2},{1,31},{2,4},{3,1},{4,6},{5,3},{6,8},{7,5},{8,10},{9,7},{10,... | collective-permute-start | bytes 442376 | tf_op jit(solution)/shard_map/ppermute | solution.py:365
  48.0 3.1 %collective-permute-start.5 = (bf16[288,256]{1,0:T(8,128)(2,1)S(1)}, bf16[288,256]{1,0:T(8,128)(2,1)S(1)}, u32[]{:S(2)}, u32[]{:S(2)}) collective-permute-start(bf16[288,256]{1,0:T(8,128)(2,1)S(1)} %collective-permute-done.4.refs_0_), channel_id=1, source_target_pairs={{0,2},{1,31},{2,4},{3,1},{4,6},{5,3},{6,8},{7,5},{8,10},{9,7},{10,... | collective-permute-start | bytes 442376 | tf_op jit(solution)/shard_map/ppermute | solution.py:365
  53.4 2.9 %collective-permute-start.6 = (bf16[288,256]{1,0:T(8,128)(2,1)S(1)}, bf16[288,256]{1,0:T(8,128)(2,1)S(1)}, u32[]{:S(2)}, u32[]{:S(2)}) collective-permute-start(bf16[288,256]{1,0:T(8,128)(2,1)S(1)} %collective-permute-done.5.refs_0_), channel_id=1, source_target_pairs={{0,2},{1,31},{2,4},{3,1},{4,6},{5,3},{6,8},{7,5},{8,10},{9,7},{10,... | collective-permute-start | bytes 442376 | tf_op jit(solution)/shard_map/ppermute | solution.py:365
  57.9 3.0 %attention_first.1 = (f32[9,128,256]{2,1,0:T(8,128)S(1)}, f32[8,8,256]{2,1,0:T(8,128)S(1)}, f32[16,384]{1,0:T(8,128)S(1)}) custom-call(s32[4]{0:T(128)S(1)} %get-tuple-element.51.where_ref, s32[256]{0:T(256)S(1)} %reshape.22.offset_ref, s32[256]{0:T(256)S(1)} %reshape.23.count_ref, bf16[288,256]{1,0:T(8,128)(2,1)S(1)} %constant_dynamic-update-slice_fusion.4.refs_0_, ...), custom_call_target="tpu_custom_call" | custom-call | flops 603979776 | bytes 4194304 | tf_op jit(solution)/shard_map/attention_first/pallas_call | solution.py:267
  62.2 3.0 %collective-permute-start.7 = (bf16[288,256]{1,0:T(8,128)(2,1)S(1)}, bf16[288,256]{1,0:T(8,128)(2,1)S(1)}, u32[]{:S(2)}, u32[]{:S(2)}) collective-permute-start(bf16[288,256]{1,0:T(8,128)(2,1)S(1)} %collective-permute-done.6.refs_0_), channel_id=1, source_target_pairs={{0,2},{1,31},{2,4},{3,1},{4,6},{5,3},{6,8},{7,5},{8,10},{9,7},{10,... | collective-permute-start | bytes 442376 | tf_op jit(solution)/shard_map/ppermute | solution.py:365
  65.4 4.5 %attention.7 = (f32[9,128,256]{2,1,0:T(8,128)S(1)}, f32[8,8,256]{2,1,0:T(8,128)S(1)}, f32[16,384]{1,0:T(8,128)S(1)}) custom-call(s32[4]{0:T(128)S(1)} %get-tuple-element.50.where_ref, s32[256]{0:T(256)S(1)} %reshape.22.offset_ref, s32[256]{0:T(256)S(1)} %reshape.23.count_ref, ...), custom_call_target="tpu_custom_call", output_to_operand_aliasing={{0}: (8, {}), {1}: (9, {}), {2}: (10, {})} | custom-call | flops 1207959552 | bytes 4194304 | tf_op jit(solution)/shard_map/attention/pallas_call | solution.py:267
  69.8 4.5 %attention.8 = (f32[9,128,256]{2,1,0:T(8,128)S(1)}, f32[8,8,256]{2,1,0:T(8,128)S(1)}, f32[16,384]{1,0:T(8,128)S(1)}) custom-call(s32[4]{0:T(128)S(1)} %add.75.where_ref, s32[256]{0:T(256)S(1)} %reshape.22.offset_ref, s32[256]{0:T(256)S(1)} %reshape.23.count_ref, ...), custom_call_target="tpu_custom_call", output_to_operand_aliasing={{0}: (8, {}), {1}: (9, {}), {2}: (10, {})} | custom-call | flops 1207959552 | bytes 4194304 | tf_op jit(solution)/shard_map/attention/pallas_call | solution.py:267
  75.5 2.9 %collective-permute-done.8.refs_0_ = bf16[288,256]{1,0:T(8,128)(2,1)S(1)} collective-permute-done((bf16[288,256]{1,0:T(8,128)(2,1)S(1)}, bf16[288,256]{1,0:T(8,128)(2,1)S(1)}, u32[]{:S(2)}, u32[]{:S(2)}) %collective-permute-start.8) | collective-permute-done | bytes 147488 | tf_op jit(solution)/shard_map/ppermute | solution.py:365
  81.3 4.5 %attention.9 = (f32[9,128,256]{2,1,0:T(8,128)S(1)}, f32[8,8,256]{2,1,0:T(8,128)S(1)}, f32[16,384]{1,0:T(8,128)S(1)}) custom-call(s32[4]{0:T(128)S(1)} %add.76.where_ref, s32[256]{0:T(256)S(1)} %reshape.22.offset_ref, s32[256]{0:T(256)S(1)} %reshape.23.count_ref, ...), custom_call_target="tpu_custom_call", output_to_operand_aliasing={{0}: (8, {}), {1}: (9, {}), {2}: (10, {})} | custom-call | flops 1207959552 | bytes 4194304 | tf_op jit(solution)/shard_map/attention/pallas_call | solution.py:267
  87.1 3.0 %collective-permute-start.10 = (bf16[288,256]{1,0:T(8,128)(2,1)S(1)}, bf16[288,256]{1,0:T(8,128)(2,1)S(1)}, u32[]{:S(2)}, u32[]{:S(2)}) collective-permute-start(bf16[288,256]{1,0:T(8,128)(2,1)S(1)} %collective-permute-done.9.refs_0_), channel_id=1, source_target_pairs={{0,2},{1,31},{2,4},{3,1},{4,6},{5,3},{6,8},{7,5},{8,10},{9,7},{10,... | collective-permute-start | bytes 442376 | tf_op jit(solution)/shard_map/ppermute | solution.py:365
  90.2 4.5 %attention.10 = (f32[9,128,256]{2,1,0:T(8,128)S(1)}, f32[8,8,256]{2,1,0:T(8,128)S(1)}, f32[16,384]{1,0:T(8,128)S(1)}) custom-call(s32[4]{0:T(128)S(1)} %add.77.where_ref, s32[256]{0:T(256)S(1)} %reshape.22.offset_ref, s32[256]{0:T(256)S(1)} %reshape.23.count_ref, ...), custom_call_target="tpu_custom_call", output_to_operand_aliasing={{0}: (8, {}), {1}: (9, {}), {2}: (10, {})} | custom-call | flops 1207959552 | bytes 4194304 | tf_op jit(solution)/shard_map/attention/pallas_call | solution.py:267
  95.3 4.5 %attention.11 = (f32[9,128,256]{2,1,0:T(8,128)S(1)}, f32[8,8,256]{2,1,0:T(8,128)S(1)}, f32[16,384]{1,0:T(8,128)S(1)}) custom-call(s32[4]{0:T(128)S(1)} %add.78.where_ref, s32[256]{0:T(256)S(1)} %reshape.22.offset_ref, s32[256]{0:T(256)S(1)} %reshape.23.count_ref, ...), custom_call_target="tpu_custom_call", output_to_operand_aliasing={{0}: (8, {}), {1}: (9, {}), {2}: (10, {})} | custom-call | flops 1207959552 | bytes 4194304 | tf_op jit(solution)/shard_map/attention/pallas_call | solution.py:267
  99.8 4.5 %attention.12 = (f32[9,128,256]{2,1,0:T(8,128)S(1)}, f32[8,8,256]{2,1,0:T(8,128)S(1)}, f32[16,384]{1,0:T(8,128)S(1)}) custom-call(s32[4]{0:T(128)S(1)} %add.79.where_ref, s32[256]{0:T(256)S(1)} %reshape.22.offset_ref, s32[256]{0:T(256)S(1)} %reshape.23.count_ref, ...), custom_call_target="tpu_custom_call", output_to_operand_aliasing={{0}: (8, {}), {1}: (9, {}), {2}: (10, {})} | custom-call | flops 1207959552 | bytes 4194304 | tf_op jit(solution)/shard_map/attention/pallas_call | solution.py:267
  104.3 4.5 %attention.13 = (f32[9,128,256]{2,1,0:T(8,128)S(1)}, f32[8,8,256]{2,1,0:T(8,128)S(1)}, f32[16,384]{1,0:T(8,128)S(1)}) custom-call(s32[4]{0:T(128)S(1)} %add.80.where_ref, s32[256]{0:T(256)S(1)} %reshape.22.offset_ref, s32[256]{0:T(256)S(1)} %reshape.23.count_ref, ...), custom_call_target="tpu_custom_call", output_to_operand_aliasing={{0}: (8, {}), {1}: (9, {}), {2}: (10, {})} | custom-call | flops 1207959552 | bytes 4194304 | tf_op jit(solution)/shard_map/attention/pallas_call | solution.py:267
  108.8 3.5 %attention_last.1 = bf16[4,72,1024]{2,1,0:T(8,128)(2,1)S(1)} custom-call(s32[4]{0:T(128)S(1)} %add.81.where_ref, s32[256]{0:T(256)S(1)} %reshape.22.offset_ref, s32[256]{0:T(256)S(1)} %reshape.23.count_ref, bf16[288,256]{1,0:T(8,128)(2,1)S(1)} %collective-permute-done.10.refs_0_, bf16[288,256]{1,0:T(8,128)(2,1)S(1)} %collective-permute-done.11.refs_1_, ...), custom_call_target="tpu_custom_call" | custom-call | flops 603979776 | bytes 4194304 | tf_op jit(solution)/shard_map/attention_last/pallas_call | solution.py:267
  112.5 1.7 %collective-permute-start.31 = (bf16[72,1024]{1,0:T(8,128)(2,1)S(1)}, bf16[72,1024]{1,0:T(8,128)(2,1)S(1)}, u32[]{:S(2)}, u32[]{:S(2)}) collective-permute-start(bf16[72,1024]{1,0:T(8,128)(2,1)S(1)} %get-tuple-element.53), channel_id=1, source_target_pairs={{0,64},{32,96},{64,0},{96,32},{1,65},{33,97},{65,1},{97,33},{2,66}... | collective-permute-start | bytes 442376 | tf_op jit(solution)/shard_map/ppermute | solution.py:400
  115.1 2.8 %collective-permute-done.30 = bf16[72,1024]{1,0:T(8,128)(2,1)S(1)} collective-permute-done((bf16[72,1024]{1,0:T(8,128)(2,1)S(1)}, bf16[72,1024]{1,0:T(8,128)(2,1)S(1)}, u32[]{:S(2)}, u32[]{:S(2)}) %collective-permute-start.30) | collective-permute-done | bytes 147488 | tf_op jit(solution)/shard_map/ppermute | solution.py:400
  119.5 3.6 %collective-permute-done.32 = bf16[72,1024]{1,0:T(8,128)(2,1)S(1)} collective-permute-done((bf16[72,1024]{1,0:T(8,128)(2,1)S(1)}, bf16[72,1024]{1,0:T(8,128)(2,1)S(1)}, u32[]{:S(2)}, u32[]{:S(2)}) %collective-permute-start.32) | collective-permute-done | bytes 147488 | tf_op jit(solution)/shard_map/ppermute | solution.py:400
  (120 shorter events, 22.7 us)
Async XLA Ops:
  3.9 8.5 %collective-permute-start.2 = (bf16[72,256]{1,0:T(8,128)(2,1)S(1)}, bf16[72,256]{1,0:T(8,128)(2,1)S(1)}, u32[]{:S(2)}, u32[]{:S(2)}) collective-permute-start(bf16[72,256]{1,0:T(8,128)(2,1)S(1)} %pad_maximum_fusion.10), channel_id=1, source_target_pairs={{0,96},{32,0},{64,32},{96,64},{1,97},{33,1},{65,33},{97,65},{2,98}... | collective-permute-start | bytes 110600 | tf_op jit(solution)/shard_map/ppermute | solution.py:333
  12.6 27.8 %collective-permute-start.15 = (bf16[288,256]{1,0:T(8,128)(2,1)S(1)}, bf16[288,256]{1,0:T(8,128)(2,1)S(1)}, u32[]{:S(2)}, u32[]{:S(2)}) collective-permute-start(bf16[288,256]{1,0:T(8,128)(2,1)S(1)} %constant_dynamic-update-slice_fusion.4.refs_0_), channel_id=1, source_target_pairs={{0,1},{1,0},{2,3},{3,2},{4,5},{5,4},{6,7},{7,6},{8,9},{9,8},{10,11... | collective-permute-start | bytes 442376 | tf_op jit(solution)/shard_map/ppermute | solution.py:368
  31.4 21.3 %collective-permute-start.12 = (bf16[64,1024]{1,0:T(8,128)(2,1)S(1)}, bf16[64,1024]{1,0:T(8,128)(2,1)S(1)}, u32[]{:S(2)}, u32[]{:S(2)}) collective-permute-start(bf16[64,1024]{1,0:T(8,128)(2,1)S(1)} %get-tuple-element.56), channel_id=1, source_target_pairs={{0,32},{32,64},{64,96},{96,0},{1,33},{33,65},{65,97},{97,1},{2,34}... | collective-permute-start | bytes 393224 | tf_op jit(solution)/shard_map/ppermute | solution.py:341
  32.0 20.8 %collective-permute-start.13 = (bf16[64,1024]{1,0:T(8,128)(2,1)S(1)}, bf16[64,1024]{1,0:T(8,128)(2,1)S(1)}, u32[]{:S(2)}, u32[]{:S(2)}) collective-permute-start(bf16[64,1024]{1,0:T(8,128)(2,1)S(1)} %get-tuple-element.58), channel_id=1, source_target_pairs={{0,64},{32,96},{64,0},{96,32},{1,65},{33,97},{65,1},{97,33},{2,66}... | collective-permute-start | bytes 393224 | tf_op jit(solution)/shard_map/ppermute | solution.py:341
  34.4 19.0 %collective-permute-start.14 = (bf16[64,1024]{1,0:T(8,128)(2,1)S(1)}, bf16[64,1024]{1,0:T(8,128)(2,1)S(1)}, u32[]{:S(2)}, u32[]{:S(2)}) collective-permute-start(bf16[64,1024]{1,0:T(8,128)(2,1)S(1)} %get-tuple-element.57), channel_id=1, source_target_pairs={{0,96},{32,0},{64,32},{96,64},{1,97},{33,1},{65,33},{97,65},{2,98}... | collective-permute-start | bytes 393224 | tf_op jit(solution)/shard_map/ppermute | solution.py:341
  34.6 7.9 %collective-permute-start.3 = (bf16[288,256]{1,0:T(8,128)(2,1)S(1)}, bf16[288,256]{1,0:T(8,128)(2,1)S(1)}, u32[]{:S(2)}, u32[]{:S(2)}) collective-permute-start(bf16[288,256]{1,0:T(8,128)(2,1)S(1)} %constant_dynamic-update-slice_fusion.4.refs_0_), channel_id=1, source_target_pairs={{0,2},{1,31},{2,4},{3,1},{4,6},{5,3},{6,8},{7,5},{8,10},{9,7},{10,... | collective-permute-start | bytes 442376 | tf_op jit(solution)/shard_map/ppermute | solution.py:365
  52.7 12.6 %collective-permute-start.29 = (bf16[576,256]{1,0:T(8,128)(2,1)S(1)}, bf16[576,256]{1,0:T(8,128)(2,1)S(1)}, u32[]{:S(2)}, u32[]{:S(2)}) collective-permute-start(bf16[576,256]{1,0:T(8,128)(2,1)S(1)} %pad_maximum_fusion.7), channel_id=1, source_target_pairs={{0,1},{1,0},{2,3},{3,2},{4,5},{5,4},{6,7},{7,6},{8,9},{9,8},{10,11... | collective-permute-start | bytes 884744 | tf_op jit(solution)/shard_map/ppermute | solution.py:368
  52.9 17.0 %collective-permute-start.28 = (bf16[576,256]{1,0:T(8,128)(2,1)S(1)}, bf16[576,256]{1,0:T(8,128)(2,1)S(1)}, u32[]{:S(2)}, u32[]{:S(2)}) collective-permute-start(bf16[576,256]{1,0:T(8,128)(2,1)S(1)} %pad_maximum_fusion.6), channel_id=1, source_target_pairs={{0,1},{1,0},{2,3},{3,2},{4,5},{5,4},{6,7},{7,6},{8,9},{9,8},{10,11... | collective-permute-start | bytes 884744 | tf_op jit(solution)/shard_map/ppermute | solution.py:368
  53.4 8.8 %collective-permute-start.6 = (bf16[288,256]{1,0:T(8,128)(2,1)S(1)}, bf16[288,256]{1,0:T(8,128)(2,1)S(1)}, u32[]{:S(2)}, u32[]{:S(2)}) collective-permute-start(bf16[288,256]{1,0:T(8,128)(2,1)S(1)} %collective-permute-done.5.refs_0_), channel_id=1, source_target_pairs={{0,2},{1,31},{2,4},{3,1},{4,6},{5,3},{6,8},{7,5},{8,10},{9,7},{10,... | collective-permute-start | bytes 442376 | tf_op jit(solution)/shard_map/ppermute | solution.py:365
  56.3 8.9 %collective-permute-start.19 = (bf16[288,256]{1,0:T(8,128)(2,1)S(1)}, bf16[288,256]{1,0:T(8,128)(2,1)S(1)}, u32[]{:S(2)}, u32[]{:S(2)}) collective-permute-start(bf16[288,256]{1,0:T(8,128)(2,1)S(1)} %collective-permute-done.18.refs_1_), channel_id=1, source_target_pairs={{0,2},{1,31},{2,4},{3,1},{4,6},{5,3},{6,8},{7,5},{8,10},{9,7},{10,... | collective-permute-start | bytes 442376 | tf_op jit(solution)/shard_map/ppermute | solution.py:365
  61.0 20.4 %collective-permute-start.27 = (bf16[576,256]{1,0:T(8,128)(2,1)S(1)}, bf16[576,256]{1,0:T(8,128)(2,1)S(1)}, u32[]{:S(2)}, u32[]{:S(2)}) collective-permute-start(bf16[576,256]{1,0:T(8,128)(2,1)S(1)} %pad_maximum_fusion.5), channel_id=1, source_target_pairs={{0,1},{1,0},{2,3},{3,2},{4,5},{5,4},{6,7},{7,6},{8,9},{9,8},{10,11... | collective-permute-start | bytes 884744 | tf_op jit(solution)/shard_map/ppermute | solution.py:368
  62.2 12.2 %collective-permute-start.7 = (bf16[288,256]{1,0:T(8,128)(2,1)S(1)}, bf16[288,256]{1,0:T(8,128)(2,1)S(1)}, u32[]{:S(2)}, u32[]{:S(2)}) collective-permute-start(bf16[288,256]{1,0:T(8,128)(2,1)S(1)} %collective-permute-done.6.refs_0_), channel_id=1, source_target_pairs={{0,2},{1,31},{2,4},{3,1},{4,6},{5,3},{6,8},{7,5},{8,10},{9,7},{10,... | collective-permute-start | bytes 442376 | tf_op jit(solution)/shard_map/ppermute | solution.py:365
  65.2 9.4 %collective-permute-start.20 = (bf16[288,256]{1,0:T(8,128)(2,1)S(1)}, bf16[288,256]{1,0:T(8,128)(2,1)S(1)}, u32[]{:S(2)}, u32[]{:S(2)}) collective-permute-start(bf16[288,256]{1,0:T(8,128)(2,1)S(1)} %collective-permute-done.19.refs_1_), channel_id=1, source_target_pairs={{0,2},{1,31},{2,4},{3,1},{4,6},{5,3},{6,8},{7,5},{8,10},{9,7},{10,... | collective-permute-start | bytes 442376 | tf_op jit(solution)/shard_map/ppermute | solution.py:365
  74.6 5.7 %collective-permute-start.21 = (bf16[288,256]{1,0:T(8,128)(2,1)S(1)}, bf16[288,256]{1,0:T(8,128)(2,1)S(1)}, u32[]{:S(2)}, u32[]{:S(2)}) collective-permute-start(bf16[288,256]{1,0:T(8,128)(2,1)S(1)} %collective-permute-done.20.refs_1_), channel_id=1, source_target_pairs={{0,2},{1,31},{2,4},{3,1},{4,6},{5,3},{6,8},{7,5},{8,10},{9,7},{10,... | collective-permute-start | bytes 442376 | tf_op jit(solution)/shard_map/ppermute | solution.py:365
  74.7 15.5 %collective-permute-start.26 = (bf16[576,256]{1,0:T(8,128)(2,1)S(1)}, bf16[576,256]{1,0:T(8,128)(2,1)S(1)}, u32[]{:S(2)}, u32[]{:S(2)}) collective-permute-start(bf16[576,256]{1,0:T(8,128)(2,1)S(1)} %pad_maximum_fusion.4), channel_id=1, source_target_pairs={{0,1},{1,0},{2,3},{3,2},{4,5},{5,4},{6,7},{7,6},{8,9},{9,8},{10,11... | collective-permute-start | bytes 884744 | tf_op jit(solution)/shard_map/ppermute | solution.py:368
  74.9 20.4 %collective-permute-start.25 = (bf16[576,256]{1,0:T(8,128)(2,1)S(1)}, bf16[576,256]{1,0:T(8,128)(2,1)S(1)}, u32[]{:S(2)}, u32[]{:S(2)}) collective-permute-start(bf16[576,256]{1,0:T(8,128)(2,1)S(1)} %pad_maximum_fusion.3), channel_id=1, source_target_pairs={{0,1},{1,0},{2,3},{3,2},{4,5},{5,4},{6,7},{7,6},{8,9},{9,8},{10,11... | collective-permute-start | bytes 884744 | tf_op jit(solution)/shard_map/ppermute | solution.py:368
  78.4 8.7 %collective-permute-start.9 = (bf16[288,256]{1,0:T(8,128)(2,1)S(1)}, bf16[288,256]{1,0:T(8,128)(2,1)S(1)}, u32[]{:S(2)}, u32[]{:S(2)}) collective-permute-start(bf16[288,256]{1,0:T(8,128)(2,1)S(1)} %collective-permute-done.8.refs_0_), channel_id=1, source_target_pairs={{0,2},{1,31},{2,4},{3,1},{4,6},{5,3},{6,8},{7,5},{8,10},{9,7},{10,... | collective-permute-start | bytes 442376 | tf_op jit(solution)/shard_map/ppermute | solution.py:365
  80.3 9.7 %collective-permute-start.22 = (bf16[288,256]{1,0:T(8,128)(2,1)S(1)}, bf16[288,256]{1,0:T(8,128)(2,1)S(1)}, u32[]{:S(2)}, u32[]{:S(2)}) collective-permute-start(bf16[288,256]{1,0:T(8,128)(2,1)S(1)} %collective-permute-done.21.refs_1_), channel_id=1, source_target_pairs={{0,2},{1,31},{2,4},{3,1},{4,6},{5,3},{6,8},{7,5},{8,10},{9,7},{10,... | collective-permute-start | bytes 442376 | tf_op jit(solution)/shard_map/ppermute | solution.py:365
  85.9 13.9 %collective-permute-start.24 = (bf16[576,256]{1,0:T(8,128)(2,1)S(1)}, bf16[576,256]{1,0:T(8,128)(2,1)S(1)}, u32[]{:S(2)}, u32[]{:S(2)}) collective-permute-start(bf16[576,256]{1,0:T(8,128)(2,1)S(1)} %pad_maximum_fusion.2), channel_id=1, source_target_pairs={{0,1},{1,0},{2,3},{3,2},{4,5},{5,4},{6,7},{7,6},{8,9},{9,8},{10,11... | collective-permute-start | bytes 884744 | tf_op jit(solution)/shard_map/ppermute | solution.py:368
  87.1 7.6 %collective-permute-start.10 = (bf16[288,256]{1,0:T(8,128)(2,1)S(1)}, bf16[288,256]{1,0:T(8,128)(2,1)S(1)}, u32[]{:S(2)}, u32[]{:S(2)}) collective-permute-start(bf16[288,256]{1,0:T(8,128)(2,1)S(1)} %collective-permute-done.9.refs_0_), channel_id=1, source_target_pairs={{0,2},{1,31},{2,4},{3,1},{4,6},{5,3},{6,8},{7,5},{8,10},{9,7},{10,... | collective-permute-start | bytes 442376 | tf_op jit(solution)/shard_map/ppermute | solution.py:365
  90.1 14.2 %collective-permute-start.23 = (bf16[576,256]{1,0:T(8,128)(2,1)S(1)}, bf16[576,256]{1,0:T(8,128)(2,1)S(1)}, u32[]{:S(2)}, u32[]{:S(2)}) collective-permute-start(bf16[576,256]{1,0:T(8,128)(2,1)S(1)} %pad_maximum_fusion.1), channel_id=1, source_target_pairs={{0,1},{1,0},{2,3},{3,2},{4,5},{5,4},{6,7},{7,6},{8,9},{9,8},{10,11... | collective-permute-start | bytes 884744 | tf_op jit(solution)/shard_map/ppermute | solution.py:368
  94.7 14.1 %collective-permute-start.11 = (bf16[288,256]{1,0:T(8,128)(2,1)S(1)}, bf16[288,256]{1,0:T(8,128)(2,1)S(1)}, u32[]{:S(2)}, u32[]{:S(2)}) collective-permute-start(bf16[288,256]{1,0:T(8,128)(2,1)S(1)} %collective-permute-done.10.refs_0_), channel_id=1, source_target_pairs={{0,1},{1,0},{2,3},{3,2},{4,5},{5,4},{6,7},{7,6},{8,9},{9,8},{10,11... | collective-permute-start | bytes 442376 | tf_op jit(solution)/shard_map/ppermute | solution.py:368
  112.5 7.0 %collective-permute-start.31 = (bf16[72,1024]{1,0:T(8,128)(2,1)S(1)}, bf16[72,1024]{1,0:T(8,128)(2,1)S(1)}, u32[]{:S(2)}, u32[]{:S(2)}) collective-permute-start(bf16[72,1024]{1,0:T(8,128)(2,1)S(1)} %get-tuple-element.53), channel_id=1, source_target_pairs={{0,64},{32,96},{64,0},{96,32},{1,65},{33,97},{65,1},{97,33},{2,66}... | collective-permute-start | bytes 442376 | tf_op jit(solution)/shard_map/ppermute | solution.py:400
  114.3 8.8 %collective-permute-start.32 = (bf16[72,1024]{1,0:T(8,128)(2,1)S(1)}, bf16[72,1024]{1,0:T(8,128)(2,1)S(1)}, u32[]{:S(2)}, u32[]{:S(2)}) collective-permute-start(bf16[72,1024]{1,0:T(8,128)(2,1)S(1)} %get-tuple-element.52), channel_id=1, source_target_pairs={{0,32},{32,64},{64,96},{96,0},{1,33},{33,65},{65,97},{97,1},{2,34}... | collective-permute-start | bytes 442376 | tf_op jit(solution)/shard_map/ppermute | solution.py:400
  (16 other events, 348.0 us)
where the time goes:
time: 125 us
  starting transfers between devices  62.3 us (50%)
  Pallas kernels  38.1 us (30%)
  waiting for transfers between devices  17.3 us (14%)
  local copies, waits for them, and re-layouts  5.41 us (4%)
    pallas_call x9, Pallas kernels, run_step(): pl.pallas_call(kernel, out_shape=out_shape, in_specs=[smem] * 3 + [vmem]...  38.1 us
    ppermute x15, starting transfers between devices, pass_on(): return lax.ppermute(block, RING, ring)  28.4 us
    ppermute x9, starting transfers between devices, swap(): return lax.ppermute(block, 'ctx_2', rotation(CORES, 1))  23.3 us
    ppermute x3, waiting for transfers between devices, body(): back.append(lax.ppermute(out[by], 'ctx_0', rotation(COLUMNS, -by)))  7.98 us
    ppermute x15, waiting for transfers between devices, pass_on(): return lax.ppermute(block, RING, ring)  5.58 us
    ppermute x3, starting transfers between devices, body(): lax.ppermute(key_value_of(heads_at(by)), 'ctx_0', rotation(COLUMNS, by))  4.81 us
    ppermute x3, waiting for transfers between devices, body(): lax.ppermute(key_value_of(heads_at(by)), 'ctx_0', rotation(COLUMNS, by))  3.71 us
    ppermute x3, starting transfers between devices, body(): queries.append(lax.ppermute(mine, 'ctx_0', rotation(COLUMNS, by)))  3.19 us
  transfers between devices with their start and end apart: 33, of which 8 were waited for; matrix products, arithmetic and copies ran while one was open for 1% of the time, Pallas kernels for 28%

commit v1 on v0

--- a/solution.py
+++ b/solution.py
@@ -226,10 +226,7 @@
         numerator = keep * mixture + own_weight * decode_value_ref[...].astype(jnp.float32)
         result = numerator / (keep * totals + own_weight)
         for column in range(COLUMNS):
-            for h in range(HEADS_PER_GROUP):
-                out_ref[column, 2 * HALF : 2 * HALF + 8, h * HEAD_WIDTH : (h + 1) * HEAD_WIDTH] = (
-                    jnp.broadcast_to(result[h : h + 1, :], (8, HEAD_WIDTH)).astype(jnp.bfloat16)
-                )
+            out_ref[column, 2 * HALF :, :HEAD_WIDTH] = result[:HEADS_PER_GROUP, :].astype(jnp.bfloat16)
     else:
         decode_out[:, :HEAD_WIDTH] = mixture
         decode_out[:, HEAD_WIDTH : 2 * HEAD_WIDTH] = jnp.broadcast_to(peak, mixture.shape)
@@ -291,6 +288,40 @@
     )(*operands)
 
 
+def place(where_ref, *refs):
+    blocks, (span_ref, next_ref, semaphores) = refs[:COLUMNS], refs[COLUMNS:]
+    copies = []
+    for by, block in enumerate(blocks):
+        head = lax.rem(where_ref[0] + by, COLUMNS)
+        columns = pl.ds(pl.multiple_of(head * GROUP_WIDTH, GROUP_WIDTH), GROUP_WIDTH)
+        rows = pl.ds(pl.multiple_of(head * HEADS_PER_GROUP, HEADS_PER_GROUP), HEADS_PER_GROUP)
+        for source, target in (
+            (block.at[: 2 * HALF, :], span_ref.at[:, columns]),
+            (block.at[2 * HALF :, :HEAD_WIDTH], next_ref.at[rows, :]),
+        ):
+            copies.append(pltpu.make_async_copy(source, target, semaphores.at[len(copies)]))
+    for copy in copies:
+        copy.start()
+    for copy in copies:
+        copy.wait()
+
+
+def run_place(where, blocks):
+    heads = COLUMNS * HEADS_PER_GROUP
+    return pl.pallas_call(
+        place,
+        out_shape=[
+            jax.ShapeDtypeStruct((2 * HALF, COLUMNS * GROUP_WIDTH), jnp.bfloat16),
+            jax.ShapeDtypeStruct((heads, HEAD_WIDTH), jnp.bfloat16),
+        ],
+        in_specs=[pl.BlockSpec(memory_space=pltpu.SMEM)] + [pl.BlockSpec(memory_space=pltpu.VMEM)] * COLUMNS,
+        out_specs=[pl.BlockSpec(memory_space=pltpu.HBM)] * 2,
+        scratch_shapes=[pltpu.SemaphoreType.DMA((2 * COLUMNS,))],
+        compiler_params=pltpu.CompilerParams(vmem_limit_bytes=8 << 20),
+        name="place",
+    )(where, *blocks)
+
+
 def rotation(size, by):
     return [(i, (i + by) % size) for i in range(size)]
 
@@ -314,15 +345,23 @@
     counts = shard_counts.reshape(-1)
 
     def key_value_of(head):
-        keys = jnp.concatenate([prompt_key, prefix_key_cache], 0)
-        values = jnp.concatenate([prompt_value, prefix_value_cache], 0)
-        at = head * HEAD_WIDTH
-        return jnp.concatenate(
-            [
-                lax.dynamic_slice_in_dim(keys, at, HEAD_WIDTH, 1),
-                lax.dynamic_slice_in_dim(values, at, HEAD_WIDTH, 1),
-            ],
-            1,
+        wide = (2 * HALF + PREFIX, 2 * HEAD_WIDTH)
+        slots = lax.broadcasted_iota(jnp.int32, wide, 0) < 2 * HALF
+        as_key = lax.broadcasted_iota(jnp.int32, wide, 1) < HEAD_WIDTH
+
+        def padded(array, row, column):
+            part = lax.dynamic_slice_in_dim(array, head * HEAD_WIDTH, HEAD_WIDTH, 1)
+            rows = (row, wide[0] - row - part.shape[0])
+            return jnp.pad(part, (rows, (column, wide[1] - column - HEAD_WIDTH)))
+
+        return jnp.where(
+            slots,
+            jnp.where(as_key, padded(prompt_key, 0, 0), padded(prompt_value, 0, HEAD_WIDTH)),
+            jnp.where(
+                as_key,
+                padded(prefix_key_cache, 2 * HALF, 0),
+                padded(prefix_value_cache, 2 * HALF, HEAD_WIDTH),
+            ),
         )
 
     def heads_at(by):
@@ -398,11 +437,8 @@
     back = [out[0]]
     for by in range(1, COLUMNS):
         back.append(lax.ppermute(out[by], "ctx_0", rotation(COLUMNS, -by)))
-    joined = jnp.concatenate(back + back[:-1], 1)
-    joined = lax.dynamic_slice_in_dim(
-        joined, lax.rem(COLUMNS - x, COLUMNS) * GROUP_WIDTH, COLUMNS * GROUP_WIDTH, 1
-    )
-    return joined[: 2 * HALF], joined[2 * HALF]
+    span_out, next_out = run_place(where, back)
+    return span_out, next_out.reshape(-1)
 
 
 def solution(mesh):

time: 125 us -> 123 us (0.984)
  waiting for transfers between devices: 17.3 us -> 14.2 us
  local copies, waits for them, and re-layouts: 5.41 us -> 2.35 us
  starting transfers between devices: 62.3 us -> 64.7 us
  Pallas kernels: 38.1 us -> 39.5 us
    ppermute x3, waiting for transfers between devices: 3.71 us -> 1.78 us  [body(): lax.ppermute(key_value_of(heads_at(by)), 'ctx_0', rotation(COLUMNS, by))]
    unnamed x32 -> x27, local copies, waits for them, and re-layouts: 2.09 us -> 0.29 us
    dynamic_slice x1 -> x2, local copies, waits for them, and re-layouts: 0.03 us -> 1.65 us  [padded(): part = lax.dynamic_slice_in_dim(array, head * HEAD_WIDTH, HEAD_WIDTH, 1)]
    slice x2 -> x0, local copies, waits for them, and re-layouts: 1.48 us -> none  [body(): return (joined[:2 * HALF], joined[2 * HALF])]
    pallas_call x0 -> x1, Pallas kernels: none -> 1.41 us  [run_place(): pl.pallas_call(place, out_shape=[jax.ShapeDtypeStruct((2 * HALF, COLUMNS...]
    concatenate x3 -> x0, local copies, waits for them, and re-layouts: 1.41 us -> none  [the longest x1 0.7 us: key_value_of(): values = jnp.concatenate([prompt_value, prefix_value_cache], 0)]
where the time goes in v1:
time: 123 us; the launch traced here: 122 us
  starting transfers between devices  64.7 us (53%)
  Pallas kernels  39.5 us (32%)
  waiting for transfers between devices  14.2 us (12%)
  local copies, waits for them, and re-layouts  2.35 us (2%)
    pallas_call x9, Pallas kernels, run_step(): pl.pallas_call(kernel, out_shape=out_shape, in_specs=[smem] * 3 + [vmem]...  38 us
    ppermute x15, starting transfers between devices, pass_on(): return lax.ppermute(block, RING, ring)  27.5 us
    ppermute x9, starting transfers between devices, swap(): return lax.ppermute(block, 'ctx_2', rotation(CORES, 1))  23.6 us
    ppermute x3, waiting for transfers between devices, body(): back.append(lax.ppermute(out[by], 'ctx_0', rotation(COLUMNS, -by)))  7 us
    ppermute x3, starting transfers between devices, body(): lax.ppermute(key_value_of(heads_at(by)), 'ctx_0', rotation(COLUMNS, by))  6.02 us
    ppermute x15, waiting for transfers between devices, pass_on(): return lax.ppermute(block, RING, ring)  5.42 us
    ppermute x3, starting transfers between devices, body(): queries.append(lax.ppermute(mine, 'ctx_0', rotation(COLUMNS, by)))  4.01 us
    ppermute x3, starting transfers between devices, body(): back.append(lax.ppermute(out[by], 'ctx_0', rotation(COLUMNS, -by)))  3.46 us
  transfers between devices with their start and end apart: 33, of which 8 were waited for; matrix products, arithmetic and copies ran while one was open for 1% of the time, Pallas kernels for 28%

profile of v1, /device:TPU:33, one launch (start us, length us, event | category | flops | bytes accessed | tf_op | source)
XLA Modules:
  0.0 122.4 jit_solution(13662707473016492431)
XLA Ops:
  2.5 2.3 %collective-permute-start = (bf16[72,256]{1,0:T(8,128)(2,1)S(1)}, bf16[72,256]{1,0:T(8,128)(2,1)S(1)}, u32[]{:S(2)}, u32[]{:S(2)}) collective-permute-start(bf16[72,256]{1,0:T(8,128)(2,1)S(1)} %get-tuple-element.81), channel_id=1, source_target_pairs={{0,32},{32,64},{64,96},{96,0},{1,33},{33,65},{65,97},{97,1},{2,34}... | collective-permute-start | bytes 110600 | tf_op jit(solution)/shard_map/ppermute | solution.py:372
  4.8 2.7 %collective-permute-start.1 = (bf16[72,256]{1,0:T(8,128)(2,1)S(1)}, bf16[72,256]{1,0:T(8,128)(2,1)S(1)}, u32[]{:S(2)}, u32[]{:S(2)}) collective-permute-start(bf16[72,256]{1,0:T(8,128)(2,1)S(1)} %get-tuple-element.82), channel_id=1, source_target_pairs={{0,64},{32,96},{64,0},{96,32},{1,65},{33,97},{65,1},{97,33},{2,66}... | collective-permute-start | bytes 110600 | tf_op jit(solution)/shard_map/ppermute | solution.py:372
  10.4 19.3 %collective-permute-start.15 = (bf16[288,256]{1,0:T(8,128)(2,1)S(1)}, bf16[288,256]{1,0:T(8,128)(2,1)S(1)}, u32[]{:S(2)}, u32[]{:S(2)}) collective-permute-start(bf16[288,256]{1,0:T(8,128)(2,1)S(1)} %constant_dynamic-update-slice_fusion.refs_0_), channel_id=1, source_target_pairs={{0,1},{1,0},{2,3},{3,2},{4,5},{5,4},{6,7},{7,6},{8,9},{9,8},{10,11... | collective-permute-start | bytes 442376 | tf_op jit(solution)/shard_map/ppermute | solution.py:407
  31.2 2.0 %collective-permute-start.13 = (bf16[64,1024]{1,0:T(8,128)(2,1)S(1)}, bf16[64,1024]{1,0:T(8,128)(2,1)S(1)}, u32[]{:S(2)}, u32[]{:S(2)}) collective-permute-start(bf16[64,1024]{1,0:T(8,128)(2,1)S(1)} %get-tuple-element.63), channel_id=1, source_target_pairs={{0,64},{32,96},{64,0},{96,32},{1,65},{33,97},{65,1},{97,33},{2,66}... | collective-permute-start | bytes 393224 | tf_op jit(solution)/shard_map/ppermute | solution.py:380
  33.7 4.8 %collective-permute-start.3 = (bf16[288,256]{1,0:T(8,128)(2,1)S(1)}, bf16[288,256]{1,0:T(8,128)(2,1)S(1)}, u32[]{:S(2)}, u32[]{:S(2)}) collective-permute-start(bf16[288,256]{1,0:T(8,128)(2,1)S(1)} %constant_dynamic-update-slice_fusion.refs_0_), channel_id=1, source_target_pairs={{0,2},{1,31},{2,4},{3,1},{4,6},{5,3},{6,8},{7,5},{8,10},{9,7},{10,... | collective-permute-start | bytes 442376 | tf_op jit(solution)/shard_map/ppermute | solution.py:404
  38.7 1.9 %collective-permute-done.3.refs_0_ = bf16[288,256]{1,0:T(8,128)(2,1)S(1)} collective-permute-done((bf16[288,256]{1,0:T(8,128)(2,1)S(1)}, bf16[288,256]{1,0:T(8,128)(2,1)S(1)}, u32[]{:S(2)}, u32[]{:S(2)}) %collective-permute-start.3) | collective-permute-done | bytes 147488 | tf_op jit(solution)/shard_map/ppermute | solution.py:404
  40.6 3.4 %collective-permute-start.4 = (bf16[288,256]{1,0:T(8,128)(2,1)S(1)}, bf16[288,256]{1,0:T(8,128)(2,1)S(1)}, u32[]{:S(2)}, u32[]{:S(2)}) collective-permute-start(bf16[288,256]{1,0:T(8,128)(2,1)S(1)} %collective-permute-done.3.refs_0_), channel_id=1, source_target_pairs={{0,2},{1,31},{2,4},{3,1},{4,6},{5,3},{6,8},{7,5},{8,10},{9,7},{10,... | collective-permute-start | bytes 442376 | tf_op jit(solution)/shard_map/ppermute | solution.py:404
  46.1 3.1 %collective-permute-start.5 = (bf16[288,256]{1,0:T(8,128)(2,1)S(1)}, bf16[288,256]{1,0:T(8,128)(2,1)S(1)}, u32[]{:S(2)}, u32[]{:S(2)}) collective-permute-start(bf16[288,256]{1,0:T(8,128)(2,1)S(1)} %collective-permute-done.4.refs_0_), channel_id=1, source_target_pairs={{0,2},{1,31},{2,4},{3,1},{4,6},{5,3},{6,8},{7,5},{8,10},{9,7},{10,... | collective-permute-start | bytes 442376 | tf_op jit(solution)/shard_map/ppermute | solution.py:404
  51.5 2.9 %collective-permute-start.6 = (bf16[288,256]{1,0:T(8,128)(2,1)S(1)}, bf16[288,256]{1,0:T(8,128)(2,1)S(1)}, u32[]{:S(2)}, u32[]{:S(2)}) collective-permute-start(bf16[288,256]{1,0:T(8,128)(2,1)S(1)} %collective-permute-done.5.refs_0_), channel_id=1, source_target_pairs={{0,2},{1,31},{2,4},{3,1},{4,6},{5,3},{6,8},{7,5},{8,10},{9,7},{10,... | collective-permute-start | bytes 442376 | tf_op jit(solution)/shard_map/ppermute | solution.py:404
  56.0 3.0 %attention_first.1 = (f32[9,128,256]{2,1,0:T(8,128)S(1)}, f32[8,8,256]{2,1,0:T(8,128)S(1)}, f32[16,384]{1,0:T(8,128)S(1)}) custom-call(s32[4]{0:T(128)S(1)} %get-tuple-element.55.where_ref, s32[256]{0:T(256)S(1)} %reshape.25.offset_ref, s32[256]{0:T(256)S(1)} %reshape.26.count_ref, bf16[288,256]{1,0:T(8,128)(2,1)S(1)} %constant_dynamic-update-slice_fusion.refs_0_, ...), custom_call_target="tpu_custom_call" | custom-call | flops 603979776 | bytes 4194304 | tf_op jit(solution)/shard_map/attention_first/pallas_call | solution.py:264
  60.2 3.0 %collective-permute-start.7 = (bf16[288,256]{1,0:T(8,128)(2,1)S(1)}, bf16[288,256]{1,0:T(8,128)(2,1)S(1)}, u32[]{:S(2)}, u32[]{:S(2)}) collective-permute-start(bf16[288,256]{1,0:T(8,128)(2,1)S(1)} %collective-permute-done.6.refs_0_), channel_id=1, source_target_pairs={{0,2},{1,31},{2,4},{3,1},{4,6},{5,3},{6,8},{7,5},{8,10},{9,7},{10,... | collective-permute-start | bytes 442376 | tf_op jit(solution)/shard_map/ppermute | solution.py:404
  63.4 4.5 %attention.7 = (f32[9,128,256]{2,1,0:T(8,128)S(1)}, f32[8,8,256]{2,1,0:T(8,128)S(1)}, f32[16,384]{1,0:T(8,128)S(1)}) custom-call(s32[4]{0:T(128)S(1)} %get-tuple-element.54.where_ref, s32[256]{0:T(256)S(1)} %reshape.25.offset_ref, s32[256]{0:T(256)S(1)} %reshape.26.count_ref, ...), custom_call_target="tpu_custom_call", output_to_operand_aliasing={{0}: (8, {}), {1}: (9, {}), {2}: (10, {})} | custom-call | flops 1207959552 | bytes 4194304 | tf_op jit(solution)/shard_map/attention/pallas_call | solution.py:264
  67.8 4.5 %attention.8 = (f32[9,128,256]{2,1,0:T(8,128)S(1)}, f32[8,8,256]{2,1,0:T(8,128)S(1)}, f32[16,384]{1,0:T(8,128)S(1)}) custom-call(s32[4]{0:T(128)S(1)} %add.112.where_ref, s32[256]{0:T(256)S(1)} %reshape.25.offset_ref, s32[256]{0:T(256)S(1)} %reshape.26.count_ref, ...), custom_call_target="tpu_custom_call", output_to_operand_aliasing={{0}: (8, {}), {1}: (9, {}), {2}: (10, {})} | custom-call | flops 1207959552 | bytes 4194304 | tf_op jit(solution)/shard_map/attention/pallas_call | solution.py:264
  73.5 2.9 %collective-permute-done.8.refs_0_ = bf16[288,256]{1,0:T(8,128)(2,1)S(1)} collective-permute-done((bf16[288,256]{1,0:T(8,128)(2,1)S(1)}, bf16[288,256]{1,0:T(8,128)(2,1)S(1)}, u32[]{:S(2)}, u32[]{:S(2)}) %collective-permute-start.8) | collective-permute-done | bytes 147488 | tf_op jit(solution)/shard_map/ppermute | solution.py:404
  79.3 4.5 %attention.9 = (f32[9,128,256]{2,1,0:T(8,128)S(1)}, f32[8,8,256]{2,1,0:T(8,128)S(1)}, f32[16,384]{1,0:T(8,128)S(1)}) custom-call(s32[4]{0:T(128)S(1)} %add.113.where_ref, s32[256]{0:T(256)S(1)} %reshape.25.offset_ref, s32[256]{0:T(256)S(1)} %reshape.26.count_ref, ...), custom_call_target="tpu_custom_call", output_to_operand_aliasing={{0}: (8, {}), {1}: (9, {}), {2}: (10, {})} | custom-call | flops 1207959552 | bytes 4194304 | tf_op jit(solution)/shard_map/attention/pallas_call | solution.py:264
  85.1 3.0 %collective-permute-start.10 = (bf16[288,256]{1,0:T(8,128)(2,1)S(1)}, bf16[288,256]{1,0:T(8,128)(2,1)S(1)}, u32[]{:S(2)}, u32[]{:S(2)}) collective-permute-start(bf16[288,256]{1,0:T(8,128)(2,1)S(1)} %collective-permute-done.9.refs_0_), channel_id=1, source_target_pairs={{0,2},{1,31},{2,4},{3,1},{4,6},{5,3},{6,8},{7,5},{8,10},{9,7},{10,... | collective-permute-start | bytes 442376 | tf_op jit(solution)/shard_map/ppermute | solution.py:404
  88.2 4.5 %attention.10 = (f32[9,128,256]{2,1,0:T(8,128)S(1)}, f32[8,8,256]{2,1,0:T(8,128)S(1)}, f32[16,384]{1,0:T(8,128)S(1)}) custom-call(s32[4]{0:T(128)S(1)} %add.114.where_ref, s32[256]{0:T(256)S(1)} %reshape.25.offset_ref, s32[256]{0:T(256)S(1)} %reshape.26.count_ref, ...), custom_call_target="tpu_custom_call", output_to_operand_aliasing={{0}: (8, {}), {1}: (9, {}), {2}: (10, {})} | custom-call | flops 1207959552 | bytes 4194304 | tf_op jit(solution)/shard_map/attention/pallas_call | solution.py:264
  93.3 4.5 %attention.11 = (f32[9,128,256]{2,1,0:T(8,128)S(1)}, f32[8,8,256]{2,1,0:T(8,128)S(1)}, f32[16,384]{1,0:T(8,128)S(1)}) custom-call(s32[4]{0:T(128)S(1)} %add.115.where_ref, s32[256]{0:T(256)S(1)} %reshape.25.offset_ref, s32[256]{0:T(256)S(1)} %reshape.26.count_ref, ...), custom_call_target="tpu_custom_call", output_to_operand_aliasing={{0}: (8, {}), {1}: (9, {}), {2}: (10, {})} | custom-call | flops 1207959552 | bytes 4194304 | tf_op jit(solution)/shard_map/attention/pallas_call | solution.py:264
  97.7 4.5 %attention.12 = (f32[9,128,256]{2,1,0:T(8,128)S(1)}, f32[8,8,256]{2,1,0:T(8,128)S(1)}, f32[16,384]{1,0:T(8,128)S(1)}) custom-call(s32[4]{0:T(128)S(1)} %add.116.where_ref, s32[256]{0:T(256)S(1)} %reshape.25.offset_ref, s32[256]{0:T(256)S(1)} %reshape.26.count_ref, ...), custom_call_target="tpu_custom_call", output_to_operand_aliasing={{0}: (8, {}), {1}: (9, {}), {2}: (10, {})} | custom-call | flops 1207959552 | bytes 4194304 | tf_op jit(solution)/shard_map/attention/pallas_call | solution.py:264
  102.3 4.5 %attention.13 = (f32[9,128,256]{2,1,0:T(8,128)S(1)}, f32[8,8,256]{2,1,0:T(8,128)S(1)}, f32[16,384]{1,0:T(8,128)S(1)}) custom-call(s32[4]{0:T(128)S(1)} %add.117.where_ref, s32[256]{0:T(256)S(1)} %reshape.25.offset_ref, s32[256]{0:T(256)S(1)} %reshape.26.count_ref, ...), custom_call_target="tpu_custom_call", output_to_operand_aliasing={{0}: (8, {}), {1}: (9, {}), {2}: (10, {})} | custom-call | flops 1207959552 | bytes 4194304 | tf_op jit(solution)/shard_map/attention/pallas_call | solution.py:264
  106.8 3.5 %attention_last.1 = bf16[4,72,1024]{2,1,0:T(8,128)(2,1)S(1)} custom-call(s32[4]{0:T(128)S(1)} %add.118.where_ref, s32[256]{0:T(256)S(1)} %reshape.25.offset_ref, s32[256]{0:T(256)S(1)} %reshape.26.count_ref, bf16[288,256]{1,0:T(8,128)(2,1)S(1)} %collective-permute-done.10.refs_0_, bf16[288,256]{1,0:T(8,128)(2,1)S(1)} %collective-permute-done.11.refs_1_, ...), custom_call_target="tpu_custom_call" | custom-call | flops 603979776 | bytes 4194304 | tf_op jit(solution)/shard_map/attention_last/pallas_call | solution.py:264
  110.6 3.2 %collective-permute-start.31 = (bf16[72,1024]{1,0:T(8,128)(2,1)S(1)}, bf16[72,1024]{1,0:T(8,128)(2,1)S(1)}, u32[]{:S(2)}, u32[]{:S(2)}) collective-permute-start(bf16[72,1024]{1,0:T(8,128)(2,1)S(1)} %get-tuple-element.57), channel_id=1, source_target_pairs={{0,64},{32,96},{64,0},{96,32},{1,65},{33,97},{65,1},{97,33},{2,66}... | collective-permute-start | bytes 442376 | tf_op jit(solution)/shard_map/ppermute | solution.py:439
  113.8 2.2 %collective-permute-done.30.refs_1_ = bf16[72,1024]{1,0:T(8,128)(2,1)S(1)} collective-permute-done((bf16[72,1024]{1,0:T(8,128)(2,1)S(1)}, bf16[72,1024]{1,0:T(8,128)(2,1)S(1)}, u32[]{:S(2)}, u32[]{:S(2)}) %collective-permute-start.30) | collective-permute-done | bytes 147488 | tf_op jit(solution)/shard_map/ppermute | solution.py:439
  117.7 3.1 %collective-permute-done.32.refs_3_ = bf16[72,1024]{1,0:T(8,128)(2,1)S(1)} collective-permute-done((bf16[72,1024]{1,0:T(8,128)(2,1)S(1)}, bf16[72,1024]{1,0:T(8,128)(2,1)S(1)}, u32[]{:S(2)}, u32[]{:S(2)}) %collective-permute-start.32) | collective-permute-done | bytes 147488 | tf_op jit(solution)/shard_map/ppermute | solution.py:439
  (109 shorter events, 23.4 us)
Async XLA Ops:
  2.5 6.0 %collective-permute-start = (bf16[72,256]{1,0:T(8,128)(2,1)S(1)}, bf16[72,256]{1,0:T(8,128)(2,1)S(1)}, u32[]{:S(2)}, u32[]{:S(2)}) collective-permute-start(bf16[72,256]{1,0:T(8,128)(2,1)S(1)} %get-tuple-element.81), channel_id=1, source_target_pairs={{0,32},{32,64},{64,96},{96,0},{1,33},{33,65},{65,97},{97,1},{2,34}... | collective-permute-start | bytes 110600 | tf_op jit(solution)/shard_map/ppermute | solution.py:372
  10.4 28.1 %collective-permute-start.15 = (bf16[288,256]{1,0:T(8,128)(2,1)S(1)}, bf16[288,256]{1,0:T(8,128)(2,1)S(1)}, u32[]{:S(2)}, u32[]{:S(2)}) collective-permute-start(bf16[288,256]{1,0:T(8,128)(2,1)S(1)} %constant_dynamic-update-slice_fusion.refs_0_), channel_id=1, source_target_pairs={{0,1},{1,0},{2,3},{3,2},{4,5},{5,4},{6,7},{7,6},{8,9},{9,8},{10,11... | collective-permute-start | bytes 442376 | tf_op jit(solution)/shard_map/ppermute | solution.py:407
  29.7 21.1 %collective-permute-start.12 = (bf16[64,1024]{1,0:T(8,128)(2,1)S(1)}, bf16[64,1024]{1,0:T(8,128)(2,1)S(1)}, u32[]{:S(2)}, u32[]{:S(2)}) collective-permute-start(bf16[64,1024]{1,0:T(8,128)(2,1)S(1)} %get-tuple-element.61), channel_id=1, source_target_pairs={{0,32},{32,64},{64,96},{96,0},{1,33},{33,65},{65,97},{97,1},{2,34}... | collective-permute-start | bytes 393224 | tf_op jit(solution)/shard_map/ppermute | solution.py:380
  31.2 19.8 %collective-permute-start.13 = (bf16[64,1024]{1,0:T(8,128)(2,1)S(1)}, bf16[64,1024]{1,0:T(8,128)(2,1)S(1)}, u32[]{:S(2)}, u32[]{:S(2)}) collective-permute-start(bf16[64,1024]{1,0:T(8,128)(2,1)S(1)} %get-tuple-element.63), channel_id=1, source_target_pairs={{0,64},{32,96},{64,0},{96,32},{1,65},{33,97},{65,1},{97,33},{2,66}... | collective-permute-start | bytes 393224 | tf_op jit(solution)/shard_map/ppermute | solution.py:380
  33.1 18.3 %collective-permute-start.14 = (bf16[64,1024]{1,0:T(8,128)(2,1)S(1)}, bf16[64,1024]{1,0:T(8,128)(2,1)S(1)}, u32[]{:S(2)}, u32[]{:S(2)}) collective-permute-start(bf16[64,1024]{1,0:T(8,128)(2,1)S(1)} %get-tuple-element.62), channel_id=1, source_target_pairs={{0,96},{32,0},{64,32},{96,64},{1,97},{33,1},{65,33},{97,65},{2,98}... | collective-permute-start | bytes 393224 | tf_op jit(solution)/shard_map/ppermute | solution.py:380
  33.7 6.9 %collective-permute-start.3 = (bf16[288,256]{1,0:T(8,128)(2,1)S(1)}, bf16[288,256]{1,0:T(8,128)(2,1)S(1)}, u32[]{:S(2)}, u32[]{:S(2)}) collective-permute-start(bf16[288,256]{1,0:T(8,128)(2,1)S(1)} %constant_dynamic-update-slice_fusion.refs_0_), channel_id=1, source_target_pairs={{0,2},{1,31},{2,4},{3,1},{4,6},{5,3},{6,8},{7,5},{8,10},{9,7},{10,... | collective-permute-start | bytes 442376 | tf_op jit(solution)/shard_map/ppermute | solution.py:404
  50.8 12.5 %collective-permute-start.29 = (bf16[576,256]{1,0:T(8,128)(2,1)S(1)}, bf16[576,256]{1,0:T(8,128)(2,1)S(1)}, u32[]{:S(2)}, u32[]{:S(2)}) collective-permute-start(bf16[576,256]{1,0:T(8,128)(2,1)S(1)} %pad_maximum_fusion.7), channel_id=1, source_target_pairs={{0,1},{1,0},{2,3},{3,2},{4,5},{5,4},{6,7},{7,6},{8,9},{9,8},{10,11... | collective-permute-start | bytes 884744 | tf_op jit(solution)/shard_map/ppermute | solution.py:407
  51.0 16.9 %collective-permute-start.28 = (bf16[576,256]{1,0:T(8,128)(2,1)S(1)}, bf16[576,256]{1,0:T(8,128)(2,1)S(1)}, u32[]{:S(2)}, u32[]{:S(2)}) collective-permute-start(bf16[576,256]{1,0:T(8,128)(2,1)S(1)} %pad_maximum_fusion.6), channel_id=1, source_target_pairs={{0,1},{1,0},{2,3},{3,2},{4,5},{5,4},{6,7},{7,6},{8,9},{9,8},{10,11... | collective-permute-start | bytes 884744 | tf_op jit(solution)/shard_map/ppermute | solution.py:407
  51.5 8.7 %collective-permute-start.6 = (bf16[288,256]{1,0:T(8,128)(2,1)S(1)}, bf16[288,256]{1,0:T(8,128)(2,1)S(1)}, u32[]{:S(2)}, u32[]{:S(2)}) collective-permute-start(bf16[288,256]{1,0:T(8,128)(2,1)S(1)} %collective-permute-done.5.refs_0_), channel_id=1, source_target_pairs={{0,2},{1,31},{2,4},{3,1},{4,6},{5,3},{6,8},{7,5},{8,10},{9,7},{10,... | collective-permute-start | bytes 442376 | tf_op jit(solution)/shard_map/ppermute | solution.py:404
  54.4 8.8 %collective-permute-start.19 = (bf16[288,256]{1,0:T(8,128)(2,1)S(1)}, bf16[288,256]{1,0:T(8,128)(2,1)S(1)}, u32[]{:S(2)}, u32[]{:S(2)}) collective-permute-start(bf16[288,256]{1,0:T(8,128)(2,1)S(1)} %collective-permute-done.18.refs_1_), channel_id=1, source_target_pairs={{0,2},{1,31},{2,4},{3,1},{4,6},{5,3},{6,8},{7,5},{8,10},{9,7},{10,... | collective-permute-start | bytes 442376 | tf_op jit(solution)/shard_map/ppermute | solution.py:404
  59.1 20.3 %collective-permute-start.27 = (bf16[576,256]{1,0:T(8,128)(2,1)S(1)}, bf16[576,256]{1,0:T(8,128)(2,1)S(1)}, u32[]{:S(2)}, u32[]{:S(2)}) collective-permute-start(bf16[576,256]{1,0:T(8,128)(2,1)S(1)} %pad_maximum_fusion.5), channel_id=1, source_target_pairs={{0,1},{1,0},{2,3},{3,2},{4,5},{5,4},{6,7},{7,6},{8,9},{9,8},{10,11... | collective-permute-start | bytes 884744 | tf_op jit(solution)/shard_map/ppermute | solution.py:407
  60.2 12.2 %collective-permute-start.7 = (bf16[288,256]{1,0:T(8,128)(2,1)S(1)}, bf16[288,256]{1,0:T(8,128)(2,1)S(1)}, u32[]{:S(2)}, u32[]{:S(2)}) collective-permute-start(bf16[288,256]{1,0:T(8,128)(2,1)S(1)} %collective-permute-done.6.refs_0_), channel_id=1, source_target_pairs={{0,2},{1,31},{2,4},{3,1},{4,6},{5,3},{6,8},{7,5},{8,10},{9,7},{10,... | collective-permute-start | bytes 442376 | tf_op jit(solution)/shard_map/ppermute | solution.py:404
  63.2 9.4 %collective-permute-start.20 = (bf16[288,256]{1,0:T(8,128)(2,1)S(1)}, bf16[288,256]{1,0:T(8,128)(2,1)S(1)}, u32[]{:S(2)}, u32[]{:S(2)}) collective-permute-start(bf16[288,256]{1,0:T(8,128)(2,1)S(1)} %collective-permute-done.19.refs_1_), channel_id=1, source_target_pairs={{0,2},{1,31},{2,4},{3,1},{4,6},{5,3},{6,8},{7,5},{8,10},{9,7},{10,... | collective-permute-start | bytes 442376 | tf_op jit(solution)/shard_map/ppermute | solution.py:404
  72.6 5.7 %collective-permute-start.21 = (bf16[288,256]{1,0:T(8,128)(2,1)S(1)}, bf16[288,256]{1,0:T(8,128)(2,1)S(1)}, u32[]{:S(2)}, u32[]{:S(2)}) collective-permute-start(bf16[288,256]{1,0:T(8,128)(2,1)S(1)} %collective-permute-done.20.refs_1_), channel_id=1, source_target_pairs={{0,2},{1,31},{2,4},{3,1},{4,6},{5,3},{6,8},{7,5},{8,10},{9,7},{10,... | collective-permute-start | bytes 442376 | tf_op jit(solution)/shard_map/ppermute | solution.py:404
  72.7 15.5 %collective-permute-start.26 = (bf16[576,256]{1,0:T(8,128)(2,1)S(1)}, bf16[576,256]{1,0:T(8,128)(2,1)S(1)}, u32[]{:S(2)}, u32[]{:S(2)}) collective-permute-start(bf16[576,256]{1,0:T(8,128)(2,1)S(1)} %pad_maximum_fusion.4), channel_id=1, source_target_pairs={{0,1},{1,0},{2,3},{3,2},{4,5},{5,4},{6,7},{7,6},{8,9},{9,8},{10,11... | collective-permute-start | bytes 884744 | tf_op jit(solution)/shard_map/ppermute | solution.py:407
  72.9 20.4 %collective-permute-start.25 = (bf16[576,256]{1,0:T(8,128)(2,1)S(1)}, bf16[576,256]{1,0:T(8,128)(2,1)S(1)}, u32[]{:S(2)}, u32[]{:S(2)}) collective-permute-start(bf16[576,256]{1,0:T(8,128)(2,1)S(1)} %pad_maximum_fusion.3), channel_id=1, source_target_pairs={{0,1},{1,0},{2,3},{3,2},{4,5},{5,4},{6,7},{7,6},{8,9},{9,8},{10,11... | collective-permute-start | bytes 884744 | tf_op jit(solution)/shard_map/ppermute | solution.py:407
  76.4 8.6 %collective-permute-start.9 = (bf16[288,256]{1,0:T(8,128)(2,1)S(1)}, bf16[288,256]{1,0:T(8,128)(2,1)S(1)}, u32[]{:S(2)}, u32[]{:S(2)}) collective-permute-start(bf16[288,256]{1,0:T(8,128)(2,1)S(1)} %collective-permute-done.8.refs_0_), channel_id=1, source_target_pairs={{0,2},{1,31},{2,4},{3,1},{4,6},{5,3},{6,8},{7,5},{8,10},{9,7},{10,... | collective-permute-start | bytes 442376 | tf_op jit(solution)/shard_map/ppermute | solution.py:404
  78.3 9.7 %collective-permute-start.22 = (bf16[288,256]{1,0:T(8,128)(2,1)S(1)}, bf16[288,256]{1,0:T(8,128)(2,1)S(1)}, u32[]{:S(2)}, u32[]{:S(2)}) collective-permute-start(bf16[288,256]{1,0:T(8,128)(2,1)S(1)} %collective-permute-done.21.refs_1_), channel_id=1, source_target_pairs={{0,2},{1,31},{2,4},{3,1},{4,6},{5,3},{6,8},{7,5},{8,10},{9,7},{10,... | collective-permute-start | bytes 442376 | tf_op jit(solution)/shard_map/ppermute | solution.py:404
  83.9 13.9 %collective-permute-start.24 = (bf16[576,256]{1,0:T(8,128)(2,1)S(1)}, bf16[576,256]{1,0:T(8,128)(2,1)S(1)}, u32[]{:S(2)}, u32[]{:S(2)}) collective-permute-start(bf16[576,256]{1,0:T(8,128)(2,1)S(1)} %pad_maximum_fusion.2), channel_id=1, source_target_pairs={{0,1},{1,0},{2,3},{3,2},{4,5},{5,4},{6,7},{7,6},{8,9},{9,8},{10,11... | collective-permute-start | bytes 884744 | tf_op jit(solution)/shard_map/ppermute | solution.py:407
  85.1 7.7 %collective-permute-start.10 = (bf16[288,256]{1,0:T(8,128)(2,1)S(1)}, bf16[288,256]{1,0:T(8,128)(2,1)S(1)}, u32[]{:S(2)}, u32[]{:S(2)}) collective-permute-start(bf16[288,256]{1,0:T(8,128)(2,1)S(1)} %collective-permute-done.9.refs_0_), channel_id=1, source_target_pairs={{0,2},{1,31},{2,4},{3,1},{4,6},{5,3},{6,8},{7,5},{8,10},{9,7},{10,... | collective-permute-start | bytes 442376 | tf_op jit(solution)/shard_map/ppermute | solution.py:404
  88.1 14.2 %collective-permute-start.23 = (bf16[576,256]{1,0:T(8,128)(2,1)S(1)}, bf16[576,256]{1,0:T(8,128)(2,1)S(1)}, u32[]{:S(2)}, u32[]{:S(2)}) collective-permute-start(bf16[576,256]{1,0:T(8,128)(2,1)S(1)} %pad_maximum_fusion.1), channel_id=1, source_target_pairs={{0,1},{1,0},{2,3},{3,2},{4,5},{5,4},{6,7},{7,6},{8,9},{9,8},{10,11... | collective-permute-start | bytes 884744 | tf_op jit(solution)/shard_map/ppermute | solution.py:407
  92.7 14.1 %collective-permute-start.11 = (bf16[288,256]{1,0:T(8,128)(2,1)S(1)}, bf16[288,256]{1,0:T(8,128)(2,1)S(1)}, u32[]{:S(2)}, u32[]{:S(2)}) collective-permute-start(bf16[288,256]{1,0:T(8,128)(2,1)S(1)} %collective-permute-done.10.refs_0_), channel_id=1, source_target_pairs={{0,1},{1,0},{2,3},{3,2},{4,5},{5,4},{6,7},{7,6},{8,9},{9,8},{10,11... | collective-permute-start | bytes 442376 | tf_op jit(solution)/shard_map/ppermute | solution.py:407
  110.6 7.1 %collective-permute-start.31 = (bf16[72,1024]{1,0:T(8,128)(2,1)S(1)}, bf16[72,1024]{1,0:T(8,128)(2,1)S(1)}, u32[]{:S(2)}, u32[]{:S(2)}) collective-permute-start(bf16[72,1024]{1,0:T(8,128)(2,1)S(1)} %get-tuple-element.57), channel_id=1, source_target_pairs={{0,64},{32,96},{64,0},{96,32},{1,65},{33,97},{65,1},{97,33},{2,66}... | collective-permute-start | bytes 442376 | tf_op jit(solution)/shard_map/ppermute | solution.py:439
  113.8 7.0 %collective-permute-start.32 = (bf16[72,1024]{1,0:T(8,128)(2,1)S(1)}, bf16[72,1024]{1,0:T(8,128)(2,1)S(1)}, u32[]{:S(2)}, u32[]{:S(2)}) collective-permute-start(bf16[72,1024]{1,0:T(8,128)(2,1)S(1)} %get-tuple-element.56), channel_id=1, source_target_pairs={{0,32},{32,64},{64,96},{96,0},{1,33},{33,65},{65,97},{97,1},{2,34}... | collective-permute-start | bytes 442376 | tf_op jit(solution)/shard_map/ppermute | solution.py:439
  (16 other events, 334.6 us)
